TPU v7x, 32 devices: a whole 2x2x4 slice. The times are simulated.
32 devices in a mesh: surf: 8 (over y, x, core), probe: 4 (over z).
Axes of the slice: x: 2, y: 2, z: 4, core: 2. Of those that a mesh axis runs over, the one named last changes fastest.
Arguments:
- probes: bfloat16 [32, 65536], P('probe', 'surf'), may hold values from -6 to 6
- sigma: float32 [65536], P('surf'), may hold values from 0.5 to 2
- prior_patch: bfloat16 [128, 128], replicated, may hold values from -0.5 to 0.5
- owner_map: int32 [1024], P('surf'), may hold values from 0 to 7, as said below
- block_perm: int32 [1024], P('surf'), may hold values from 0 to 127, as said below
- col_counts: int32 [1024], P('surf'), may hold values from 1 to 64
- coef: bfloat16 [1024, 1024], P('surf'), may hold values from 0.5 to 1.5
- obs_weight: bfloat16 [1024, 64], P('surf'), may hold values from 0.25 to 1
- column_op: bfloat16 [1024, 1024], replicated, may hold values from -0.1875 to 0.1875
Outputs:
- hess: float32 [32, 65536], P('probe', 'surf')
- diag_est: float32 [65536], P('surf')
- quad: float32 [32], P('probe')
Inputs may be any that keep to these rules, and one draw needn't show every extreme that they name: `owner_map`: the 128 blocks of each surface device go to 8 different column owners, 16 to each. The pairs (owner_map, block_perm) name every slot of every column owner exactly once; a column owner receives 16 blocks from each of 8 surface devices.
All inputs are finite; a program needn't handle non-finite values.
Results may differ from a plain program's by a relative error of at most 0.005.
Values may be sent and summed in bfloat16 or wider, within the bound.
No kernel may reach another device: no remote copies, remote signals or barrier semaphores. Data moves between devices by JAX's collectives and lax.ppermute only.
A program may use at most 64 MiB of HBM per device.

v0:
```python
import jax
import jax.numpy as jnp
from jax import lax
from jax.sharding import PartitionSpec as P

P_SIZE = 32
BS = 64
PATCH = 128


def column_term(fields, coef_rows, obs_rows, counts, valid, column_op):
    rows, width, cols = fields.shape
    layers = coef_rows.shape[1] // cols
    column = lax.broadcasted_iota(jnp.int32, (rows, cols), 1)
    keep = jnp.where((column < counts[:, None]) & valid[:, None], 1.0, 0.0).astype(jnp.float32)
    coef_full = (
        coef_rows.astype(jnp.float32).reshape(rows, 1, layers, cols) * keep[:, None, None, :]
    )
    lifted = (fields.astype(jnp.float32)[:, :, None, :] * coef_full).astype(jnp.bfloat16)
    state = jnp.dot(
        lifted.reshape(rows * width, layers * cols), column_op, preferred_element_type=jnp.float32
    )
    weighted = (
        state.reshape(rows, width, layers, cols) * obs_rows.astype(jnp.float32)[:, None, None, :]
    ).astype(jnp.bfloat16)
    adjoint = lax.dot_general(
        weighted.reshape(rows * width, layers * cols),
        column_op,
        (((1,), (1,)), ((), ())),
        preferred_element_type=jnp.float32,
    )
    return jnp.sum(adjoint.reshape(rows, width, layers, cols) * coef_full, axis=2)


def body(
    probes, sigma, prior_patch, owner_map, block_perm, col_counts, coef, obs_weight, column_op
):
    width, nodes = probes.shape
    blocks = owner_map.shape[0]
    peers = lax.axis_size("surf")
    depth = max(1, blocks // peers)
    slots_all = peers * depth
    grouped = probes.reshape(width, nodes // PATCH, PATCH)
    mixed = jnp.einsum("pki,ij->pkj", grouped, prior_patch, preferred_element_type=jnp.float32)
    spread = (mixed.reshape(width, nodes) * sigma[None, :]).astype(jnp.bfloat16)
    fields = spread.reshape(width, blocks, BS).transpose(1, 0, 2)
    row_ids = lax.broadcasted_iota(jnp.int32, (blocks, blocks), 0)
    col_ids = lax.broadcasted_iota(jnp.int32, (blocks, blocks), 1)
    same = (owner_map[None, :] == owner_map[:, None]) & (col_ids < row_ids)
    rank = jnp.sum(same.astype(jnp.int32), axis=1)
    position = owner_map * depth + rank
    request = (
        jnp.full((slots_all,), -1, jnp.int32).at[position].set(block_perm).reshape(peers, depth)
    )
    asked = lax.all_to_all(request, "surf", split_axis=0, concat_axis=0, tiled=True)
    wanted = asked >= 0
    safe_asked = jnp.maximum(asked, 0)
    coef_out = jnp.where(wanted[:, :, None], coef[safe_asked], jnp.zeros((), jnp.bfloat16))
    obs_out = jnp.where(wanted[:, :, None], obs_weight[safe_asked], jnp.zeros((), jnp.bfloat16))
    coef_in, obs_in = (
        lax.all_to_all(coef_out, "surf", split_axis=0, concat_axis=0, tiled=True),
        lax.all_to_all(obs_out, "surf", split_axis=0, concat_axis=0, tiled=True),
    )
    coef_rows = coef_in.reshape(slots_all, coef.shape[1])[position]
    obs_rows = obs_in.reshape(slots_all, BS)[position]
    everyone = jnp.ones((blocks,), dtype=bool)
    sens = column_term(fields, coef_rows, obs_rows, col_counts, everyone, column_op)
    sens = sens.transpose(1, 0, 2).reshape(width, nodes)
    scaled = (sens * sigma[None, :]).reshape(width, nodes // PATCH, PATCH)
    back = jnp.einsum(
        "pkj,ij->pki", scaled, prior_patch.astype(jnp.float32), precision=lax.Precision.HIGHEST
    ).reshape(width, nodes)
    values = probes.astype(jnp.float32)
    hess = values + back
    product = values * back
    diag_est = lax.psum(jnp.sum(product, axis=0), "probe") / P_SIZE
    quad = lax.psum(jnp.sum(product, axis=1), "surf")
    return (hess, diag_est, quad)


def solution(mesh):
    in_specs = (
        P("probe", "surf"),
        P("surf"),
        P(),
        P("surf"),
        P("surf"),
        P("surf"),
        P("surf", None),
        P("surf", None),
        P(),
    )
    out_specs = (P("probe", "surf"), P("surf"), P("probe"))
    return jax.shard_map(body, mesh=mesh, in_specs=in_specs, out_specs=out_specs, check_vma=False)
```

profile of v0, /device:TPU:0, one launch (start us, length us, event | category | flops | bytes accessed | tf_op | source)
XLA Modules:
  0.0 75.5 jit_solution(10636901468613469254)
XLA Ops:
  0.6 0.0 copy-start
  0.6 0.0 copy-start.6
  0.7 0.9 %convert_reduce_fusion = s32[128]{0:T(128)S(1)} fusion(s32[128]{0:T(128)} %param.12), kind=kLoop, calls=%fused_computation.21 | loop fusion | flops 81792 | bytes 1024 | tf_op jit(solution)/shard_map/reduce_sum | solution.py:50
  1.6 0.7 compare_select_fusion
  2.2 1.1 %scatter_custom_fusion = s32[128]{0:T(128)S(1)} fusion(s32[128]{0:T(128)S(1)} %compare_select_fusion, s32[128]{0:T(128)} %param.13, s32[]{:T(128)} %constant.8.clone.1), kind=kCustom, calls=%fused_computation.35 | custom fusion | bytes 1024 | tf_op jit(solution)/shard_map/scatter | solution.py:53
  3.3 0.7 all_to_all.12
  4.0 5.2 %all-to-all-start = ((s32[8,1,16]{2,1,0:T(1,128)}), s32[8,1,16]{2,1,0:T(1,128)S(1)}, u32[]{:S(2)}, u32[]{:S(2)}) async-start(s32[8,1,16]{2,1,0:T(1,128)} %bitcast.3), calls=%async_computation | async-start | bytes 8192 | tf_op jit(solution)/shard_map/all_to_all | solution.py:55
  9.2 0.8 %mul.80 = f32[128,64]{1,0:T(8,128)S(1)} reshape(f32[8192]{0:T(1024)} %param.10) | data formatting | bytes 65536 | tf_op jit(solution)/shard_map/mul | solution.py:45
  10.0 1.1 %fusion.3 = f32[8,64,128]{2,1,0:T(8,128)S(1)} fusion(bf16[8,64,128]{2,0,1:T(8,128)(2,1)} %bitcast.61, bf16[128,128]{1,0:T(8,128)(2,1)} %param.11), kind=kOutput, calls=%fused_computation.18 | convolution fusion | flops 16777216 | bytes 425984 | tf_op jit(solution)/shard_map/pki,ij->pkj/dot_general | solution.py:44
  11.1 0.1 reshape.128
  11.3 0.0 copy-done.6
  11.3 0.1 copy.60
  11.5 2.4 %all-to-all-done = s32[8,1,16]{2,1,0:T(1,128)S(1)} async-done(((s32[8,1,16]{2,1,0:T(1,128)}), s32[8,1,16]{2,1,0:T(1,128)S(1)}, u32[]{:S(2)}, u32[]{:S(2)}) %all-to-all-start) | async-done | bytes 544 | tf_op jit(solution)/shard_map/all_to_all | solution.py:55
  13.8 0.1 reshape.136
  13.9 0.7 gather_fusion.2
  14.6 0.1 broadcast_select_fusion.1
  14.7 0.7 reshape.188
  15.4 3.3 %all-to-all-start.2 = ((bf16[8,2,512]{2,1,0:T(2,128)(2,1)}), bf16[8,2,512]{2,1,0:T(2,128)(2,1)S(1)}, u32[]{:S(2)}, u32[]{:S(2)}) async-start(bf16[8,2,512]{2,1,0:T(2,128)(2,1)} %reshape.188), calls=%async_computation.2 | async-start | bytes 32768 | tf_op jit(solution)/shard_map/all_to_all | solution.py:62
  18.8 0.0 copy-done
  18.8 0.0 copy-start.1
  18.8 0.9 %gather_fusion = bf16[128,1024]{1,0:T(8,128)(2,1)S(1)} fusion(bf16[128,1024]{1,0:T(8,128)(2,1)S(1)} %copy-done, s32[1024]{0:T(1024)S(1)} %pad_clamp_fusion.1), kind=kCustom, calls=%fused_computation | custom fusion | bytes 524800 | tf_op jit(solution)/shard_map/gather | solution.py:58
  19.7 0.8 %broadcast_select_fusion = bf16[8,16,1024]{2,1,0:T(8,128)(2,1)} fusion(bf16[8,16,1024]{2,1,0:T(8,128)(2,1)S(1)} %bitcast.60, pred[8,16]{1,0:T(8,128)(4,1)S(1)} %compare_bitcast_fusion), kind=kLoop, calls=%fused_computation.15 | loop fusion | flops 131072 | bytes 524416 | tf_op jit(solution)/shard_map/jit(_where)/select_n | solution.py:58
  20.5 3.0 %all-to-all-done.2 = bf16[8,2,512]{2,1,0:T(2,128)(2,1)S(1)} async-done(((bf16[8,2,512]{2,1,0:T(2,128)(2,1)}), bf16[8,2,512]{2,1,0:T(2,128)(2,1)S(1)}, u32[]{:S(2)}, u32[]{:S(2)}) %all-to-all-start.2) | async-done | bytes 16416 | tf_op jit(solution)/shard_map/all_to_all | solution.py:62
  23.5 3.4 %all-to-all-start.1 = ((bf16[8,16,1024]{2,1,0:T(8,128)(2,1)}), bf16[8,16,1024]{2,1,0:T(8,128)(2,1)S(1)}, u32[]{:S(2)}, u32[]{:S(2)}) async-start(bf16[8,16,1024]{2,1,0:T(8,128)(2,1)} %broadcast_select_fusion), calls=%async_computation.1 | async-start | bytes 524288 | tf_op jit(solution)/shard_map/all_to_all | solution.py:61
  26.9 0.9 %copy.53 = f32[128,8,64]{0,2,1:T(8,128)} copy(f32[128,8,64]{2,0,1:T(8,128)S(1)} %convert_bitcast_fusion) | data formatting | bytes 524288 | tf_op jit(solution)/shard_map/convert_element_type | solution.py:19
  27.8 0.0 copy-done.1
  27.8 0.0 copy-start.7
  27.8 2.6 %copy.58 = bf16[1024,1024]{0,1:T(8,128)(2,1)} copy(bf16[1024,1024]{1,0:T(8,128)(2,1)S(1)} %copy-done.1) | data formatting | bytes 4194304 | tf_op args[8]
  30.4 0.0 copy-done.7
  30.4 0.1 reshape.189
  30.5 0.7 gather_fusion.3
  31.2 0.1 copy.61
  31.3 2.4 %all-to-all-done.1 = bf16[8,16,1024]{2,1,0:T(8,128)(2,1)S(1)} async-done(((bf16[8,16,1024]{2,1,0:T(8,128)(2,1)}), bf16[8,16,1024]{2,1,0:T(8,128)(2,1)S(1)}, u32[]{:S(2)}, u32[]{:S(2)}) %all-to-all-start.1) | async-done | bytes 262176 | tf_op jit(solution)/shard_map/all_to_all | solution.py:61
  33.7 0.9 %gather_fusion.1 = bf16[128,1024]{1,0:T(8,128)(2,1)S(1)} fusion(bf16[128,1024]{1,0:T(8,128)(2,1)S(1)} %bitcast.54, s32[1024]{0:T(1024)S(1)} %pad_clamp_fusion), kind=kCustom, calls=%fused_computation.1 | custom fusion | bytes 524800 | tf_op jit(solution)/shard_map/gather | solution.py:64
  34.6 0.1 copy.57
  34.7 0.0 copy-start.2
  34.8 1.7 %multiply_convert_fusion.1 = bf16[128,8,16,64]{0,3,2,1:T(8,128)(2,1)S(1)} fusion(f32[128,16,64]{0,2,1:T(8,128)S(1)} %broadcast_multiply_fusion, f32[128,8,64]{0,2,1:T(8,128)} %copy.53), kind=kLoop, calls=%fused_computation.7 | loop fusion | flops 2097152 | bytes 2883584 | tf_op jit(solution)/shard_map/convert_element_type | solution.py:19
  36.5 0.0 copy-done.2
  36.5 2.4 %multiply_convert_fusion = bf16[128,8,16,64]{0,3,2,1:T(8,128)(2,1)S(1)} fusion(bf16[128,8,1024,1]{0,2,3,1:T(8,128)(2,1)S(1)} %bitcast.58, bf16[16,64,1024,1]{2,1,0,3:T(8,128)(2,1)S(1)} %bitcast.57, f32[128,64]{0,1:T(8,128)S(1)} %convert_element_type.61), kind=kOutput, calls=%fused_computation.6 | convolution fusion | flops 2149580800 | bytes 6324224 | tf_op jit(solution)/shard_map/dot_general | solution.py:20
  38.8 0.0 copy-start.4
  38.9 0.0 copy-start.5
  38.9 2.4 %multiply_reduce_fusion = f32[128,8,64]{0,2,1:T(8,128)S(1)} fusion(bf16[128,8,1024,1]{0,2,3,1:T(8,128)(2,1)S(1)} %bitcast.67, bf16[16,64,1024,1]{2,1,0,3:T(8,128)(2,1)S(1)} %bitcast.56, f32[128,16,64]{0,2,1:T(8,128)S(1)} %broadcast_multiply_fusion), kind=kOutput, calls=%fused_computation.5 | convolution fusion | flops 2149515264 | bytes 4980736 | tf_op jit(solution)/shard_map/dot_general | solution.py:26
  41.3 0.0 copy-start.3
  41.3 0.2 copy.63
  41.5 0.1 reshape.131
  41.6 0.0 copy-done.4
  41.6 0.0 copy-done.5
  41.6 0.3 convolution_bitcast_fusion
  41.9 0.2 copy-done.3
  42.2 1.0 %fusion.1 = (f32[8]{0:T(128)S(1)}, f32[8192]{0:T(1024)S(1)}, f32[8,8192]{1,0:T(8,128)}) fusion(f32[1,8,64,128]{3,2,1,0:T(8,128)S(1)} %convolution_bitcast_fusion, bf16[8,8192]{1,0:T(8,128)(2,1)S(1)} %copy-done.3), kind=kLoop, calls=%fused_computation.16 | loop fusion | flops 319480 | bytes 688160 | tf_op jit(solution)/shard_map/reduce_sum | solution.py:77
  43.2 12.4 %psum.15 = f32[8]{0:T(128)} all-reduce(f32[8]{0:T(128)S(1)} %get-tuple-element.3), channel_id=1, replica_groups=mesh['surf'=8,'probe'=4] {'surf'}, use_global_device_ids=true, to_apply=%region_6.7 | all-reduce | flops 8 | bytes 64 | tf_op jit(solution)/shard_map/psum | solution.py:77
  55.6 19.3 %psum.14 = f32[8192]{0:T(1024)S(1)} all-reduce(f32[8192]{0:T(1024)S(1)} %get-tuple-element.4), channel_id=1, replica_groups=mesh['surf'=8,'probe'=4] {'probe'}, use_global_device_ids=true, to_apply=%region_4.5 | all-reduce | flops 8192 | bytes 65536 | tf_op jit(solution)/shard_map/psum | solution.py:76
  74.9 0.6 broadcast_multiply_fusion.1
  (8 shorter events, 0.1 us)
Async XLA Ops:
  0.6 18.2 %copy-start = (bf16[128,1024]{1,0:T(8,128)(2,1)S(1)}, bf16[128,1024]{1,0:T(8,128)(2,1)}, u32[]{:S(2)}) copy-start(bf16[128,1024]{1,0:T(8,128)(2,1)} %param.15) | copy-start | bytes 786436
  0.6 10.7 %copy-start.6 = (bf16[128,64]{0,1:T(8,128)(2,1)S(1)}, bf16[128,64]{0,1:T(8,128)(2,1)}, u32[]{:S(2)}) copy-start(bf16[128,64]{0,1:T(8,128)(2,1)} %param.16) | copy-start | bytes 49156
  4.0 9.8 %all-to-all-start = ((s32[8,1,16]{2,1,0:T(1,128)}), s32[8,1,16]{2,1,0:T(1,128)S(1)}, u32[]{:S(2)}, u32[]{:S(2)}) async-start(s32[8,1,16]{2,1,0:T(1,128)} %bitcast.3), calls=%async_computation | async-start | bytes 8192 | tf_op jit(solution)/shard_map/all_to_all | solution.py:55
  15.4 8.0 %all-to-all-start.2 = ((bf16[8,2,512]{2,1,0:T(2,128)(2,1)}), bf16[8,2,512]{2,1,0:T(2,128)(2,1)S(1)}, u32[]{:S(2)}, u32[]{:S(2)}) async-start(bf16[8,2,512]{2,1,0:T(2,128)(2,1)} %reshape.188), calls=%async_computation.2 | async-start | bytes 32768 | tf_op jit(solution)/shard_map/all_to_all | solution.py:62
  18.8 9.0 %copy-start.1 = (bf16[1024,1024]{1,0:T(8,128)(2,1)S(1)}, bf16[1024,1024]{1,0:T(8,128)(2,1)}, u32[]{:S(2)}) copy-start(bf16[1024,1024]{1,0:T(8,128)(2,1)} %param.17) | copy-start | bytes 6291460
  23.5 10.3 %all-to-all-start.1 = ((bf16[8,16,1024]{2,1,0:T(8,128)(2,1)}), bf16[8,16,1024]{2,1,0:T(8,128)(2,1)S(1)}, u32[]{:S(2)}, u32[]{:S(2)}) async-start(bf16[8,16,1024]{2,1,0:T(8,128)(2,1)} %broadcast_select_fusion), calls=%async_computation.1 | async-start | bytes 524288 | tf_op jit(solution)/shard_map/all_to_all | solution.py:61
  27.8 2.6 %copy-start.7 = (s32[128]{0:T(128)S(1)}, s32[128]{0:T(128)}, u32[]{:S(2)}) copy-start(s32[128]{0:T(128)} %param.14) | copy-start | bytes 1540
  34.7 1.7 %copy-start.2 = (bf16[1024,1024]{0,1:T(8,128)(2,1)S(1)}, bf16[1024,1024]{0,1:T(8,128)(2,1)}, u32[]{:S(2)}) copy-start(bf16[1024,1024]{0,1:T(8,128)(2,1)} %copy.58) | copy-start | bytes 6291460
  38.8 2.8 %copy-start.4 = (f32[8192]{0:T(1024)S(1)}, f32[8192]{0:T(1024)}, u32[]{:S(2)}) copy-start(f32[8192]{0:T(1024)} %param.10) | copy-start | bytes 98308
  38.9 2.8 %copy-start.5 = (bf16[128,128]{1,0:T(8,128)(2,1)S(1)}, bf16[128,128]{1,0:T(8,128)(2,1)}, u32[]{:S(2)}) copy-start(bf16[128,128]{1,0:T(8,128)(2,1)} %param.11) | copy-start | bytes 98308
  41.3 0.9 %copy-start.3 = (bf16[8,8192]{1,0:T(8,128)(2,1)S(1)}, bf16[8,8192]{1,0:T(8,128)(2,1)}, u32[]{:S(2)}) copy-start(bf16[8,8192]{1,0:T(8,128)(2,1)} %param.9) | copy-start | bytes 393220
where the time goes:
time: 76.1 us; the launch traced here: 75.5 us
  blocking collectives  31.8 us (42%)
  starting transfers between devices  11.9 us (16%)
  local copies, waits for them, and re-layouts  11.2 us (15%)
  waiting for transfers between devices  7.81 us (10%)
  matrix products  6.1 us (8%)
  other arithmetic  5.83 us (8%)
  between operations  0.9 us (1%)
    psum x1, blocking collectives, body(): diag_est = lax.psum(jnp.sum(product, axis=0), 'probe') / P_SIZE  19.3 us
    psum x1, blocking collectives, body(): quad = lax.psum(jnp.sum(product, axis=1), 'surf')  12.4 us
    all_to_all x1, starting transfers between devices, body(): lax.all_to_all(request, 'surf', split_axis=0, concat_axis=0, tiled=True)  5.2 us
    unnamed x20, local copies, waits for them, and re-layouts  3.75 us
    all_to_all x1, starting transfers between devices, body(): lax.all_to_all(coef_out, 'surf', split_axis=0, concat_axis=0, tiled=True)  3.41 us
    all_to_all x1, starting transfers between devices, body(): lax.all_to_all(obs_out, 'surf', split_axis=0, concat_axis=0, tiled=True)  3.34 us
    all_to_all x1, waiting for transfers between devices, body(): lax.all_to_all(obs_out, 'surf', split_axis=0, concat_axis=0, tiled=True)  3.01 us
    all_to_all x1, waiting for transfers between devices, body(): lax.all_to_all(coef_out, 'surf', split_axis=0, concat_axis=0, tiled=True)  2.43 us
  transfers between devices with their start and end apart: 3, of which 3 were waited for; matrix products, arithmetic and copies ran while one was open for 11% of the time, Pallas kernels for 0%

commit v1 on v0

--- a/solution.py
+++ b/solution.py
@@ -73,7 +73,7 @@
     values = probes.astype(jnp.float32)
     hess = values + back
     product = values * back
-    diag_est = lax.psum(jnp.sum(product, axis=0), "probe") / P_SIZE
+    diag_est = jnp.sum(lax.all_gather(jnp.sum(product, axis=0), "probe"), axis=0) / P_SIZE
     quad = lax.psum(jnp.sum(product, axis=1), "surf")
     return (hess, diag_est, quad)
 

time: 76.1 us -> 70.5 us (0.926)
  blocking collectives: 31.8 us -> 26 us
    psum x1 -> x0, blocking collectives: 19.3 us -> none  [body(): diag_est = lax.psum(jnp.sum(product, axis=0), 'probe') / P_SIZE]
    all_gather x0 -> x1, blocking collectives: none -> 13.6 us  [body(): lax.all_gather(jnp.sum(product, axis=0), 'probe')]
  transfers between devices with their start and end apart: 3 -> 3, of which waited for: 3 -> 3; matrix products, arithmetic and copies ran while one was open for 11% -> 12% of each run, Pallas kernels for 0% -> 0%
where the time goes in v1:
time: 70.5 us; the launch traced here: 69.9 us
  blocking collectives  26 us (37%)
  starting transfers between devices  11.9 us (17%)
  local copies, waits for them, and re-layouts  11.2 us (16%)
  waiting for transfers between devices  7.81 us (11%)
  matrix products  6.1 us (9%)
  other arithmetic  5.9 us (8%)
  between operations  0.91 us (1%)
    all_gather x1, blocking collectives, body(): lax.all_gather(jnp.sum(product, axis=0), 'probe')  13.6 us
    psum x1, blocking collectives, body(): quad = lax.psum(jnp.sum(product, axis=1), 'surf')  12.4 us
    all_to_all x1, starting transfers between devices, body(): lax.all_to_all(request, 'surf', split_axis=0, concat_axis=0, tiled=True)  5.2 us
    unnamed x20, local copies, waits for them, and re-layouts  3.75 us
    all_to_all x1, starting transfers between devices, body(): lax.all_to_all(coef_out, 'surf', split_axis=0, concat_axis=0, tiled=True)  3.41 us
    all_to_all x1, starting transfers between devices, body(): lax.all_to_all(obs_out, 'surf', split_axis=0, concat_axis=0, tiled=True)  3.34 us
    all_to_all x1, waiting for transfers between devices, body(): lax.all_to_all(obs_out, 'surf', split_axis=0, concat_axis=0, tiled=True)  3.01 us
    all_to_all x1, waiting for transfers between devices, body(): lax.all_to_all(coef_out, 'surf', split_axis=0, concat_axis=0, tiled=True)  2.43 us
  transfers between devices with their start and end apart: 3, of which 3 were waited for; matrix products, arithmetic and copies ran while one was open for 12% of the time, Pallas kernels for 0%

profile of v1, /device:TPU:0, one launch (start us, length us, event | category | flops | bytes accessed | tf_op | source)
XLA Modules:
  0.0 69.9 jit_solution(12286706464674138792)
XLA Ops:
  0.6 0.0 copy-start
  0.6 0.0 copy-start.6
  0.7 0.9 %convert_reduce_fusion = s32[128]{0:T(128)S(1)} fusion(s32[128]{0:T(128)} %param.12), kind=kLoop, calls=%fused_computation.21 | loop fusion | flops 81792 | bytes 1024 | tf_op jit(solution)/shard_map/reduce_sum | solution.py:50
  1.6 0.7 compare_select_fusion
  2.2 1.1 %scatter_custom_fusion = s32[128]{0:T(128)S(1)} fusion(s32[128]{0:T(128)S(1)} %compare_select_fusion, s32[128]{0:T(128)} %param.13, s32[]{:T(128)} %constant.8.clone.1), kind=kCustom, calls=%fused_computation.35 | custom fusion | bytes 1024 | tf_op jit(solution)/shard_map/scatter | solution.py:53
  3.3 0.7 all_to_all.12
  4.0 5.2 %all-to-all-start = ((s32[8,1,16]{2,1,0:T(1,128)}), s32[8,1,16]{2,1,0:T(1,128)S(1)}, u32[]{:S(2)}, u32[]{:S(2)}) async-start(s32[8,1,16]{2,1,0:T(1,128)} %bitcast.3), calls=%async_computation | async-start | bytes 8192 | tf_op jit(solution)/shard_map/all_to_all | solution.py:55
  9.2 0.8 %mul.80 = f32[128,64]{1,0:T(8,128)S(1)} reshape(f32[8192]{0:T(1024)} %param.10) | data formatting | bytes 65536 | tf_op jit(solution)/shard_map/mul | solution.py:45
  10.0 1.1 %fusion.3 = f32[8,64,128]{2,1,0:T(8,128)S(1)} fusion(bf16[8,64,128]{2,0,1:T(8,128)(2,1)} %bitcast.61, bf16[128,128]{1,0:T(8,128)(2,1)} %param.11), kind=kOutput, calls=%fused_computation.18 | convolution fusion | flops 16777216 | bytes 425984 | tf_op jit(solution)/shard_map/pki,ij->pkj/dot_general | solution.py:44
  11.1 0.1 reshape.128
  11.3 0.0 copy-done.6
  11.3 0.1 copy.60
  11.5 2.4 %all-to-all-done = s32[8,1,16]{2,1,0:T(1,128)S(1)} async-done(((s32[8,1,16]{2,1,0:T(1,128)}), s32[8,1,16]{2,1,0:T(1,128)S(1)}, u32[]{:S(2)}, u32[]{:S(2)}) %all-to-all-start) | async-done | bytes 544 | tf_op jit(solution)/shard_map/all_to_all | solution.py:55
  13.8 0.1 reshape.136
  13.9 0.7 %gather_fusion.2 = bf16[128,64]{1,0:T(8,128)(2,1)S(1)} fusion(bf16[128,64]{1,0:T(8,128)(2,1)S(1)} %copy.60, s32[1024]{0:T(1024)S(1)} %pad_clamp_fusion.1), kind=kCustom, calls=%fused_computation.2 | custom fusion | bytes 33280 | tf_op jit(solution)/shard_map/gather | solution.py:59
  14.6 0.1 broadcast_select_fusion.1
  14.7 0.7 %reshape.189 = bf16[8,2,512]{2,1,0:T(2,128)(2,1)} reshape(bf16[8,16,64]{2,1,0:T(8,128)(2,1)S(1)} %broadcast_select_fusion.1) | data formatting | bytes 32768
  15.4 3.3 %all-to-all-start.2 = ((bf16[8,2,512]{2,1,0:T(2,128)(2,1)}), bf16[8,2,512]{2,1,0:T(2,128)(2,1)S(1)}, u32[]{:S(2)}, u32[]{:S(2)}) async-start(bf16[8,2,512]{2,1,0:T(2,128)(2,1)} %reshape.189), calls=%async_computation.2 | async-start | bytes 32768 | tf_op jit(solution)/shard_map/all_to_all | solution.py:62
  18.8 0.0 copy-done
  18.8 0.0 copy-start.1
  18.8 0.9 %gather_fusion = bf16[128,1024]{1,0:T(8,128)(2,1)S(1)} fusion(bf16[128,1024]{1,0:T(8,128)(2,1)S(1)} %copy-done, s32[1024]{0:T(1024)S(1)} %pad_clamp_fusion.1), kind=kCustom, calls=%fused_computation | custom fusion | bytes 524800 | tf_op jit(solution)/shard_map/gather | solution.py:58
  19.7 0.8 %broadcast_select_fusion = bf16[8,16,1024]{2,1,0:T(8,128)(2,1)} fusion(bf16[8,16,1024]{2,1,0:T(8,128)(2,1)S(1)} %bitcast.60, pred[8,16]{1,0:T(8,128)(4,1)S(1)} %compare_bitcast_fusion), kind=kLoop, calls=%fused_computation.15 | loop fusion | flops 131072 | bytes 524416 | tf_op jit(solution)/shard_map/jit(_where)/select_n | solution.py:58
  20.5 3.0 %all-to-all-done.2 = bf16[8,2,512]{2,1,0:T(2,128)(2,1)S(1)} async-done(((bf16[8,2,512]{2,1,0:T(2,128)(2,1)}), bf16[8,2,512]{2,1,0:T(2,128)(2,1)S(1)}, u32[]{:S(2)}, u32[]{:S(2)}) %all-to-all-start.2) | async-done | bytes 16416 | tf_op jit(solution)/shard_map/all_to_all | solution.py:62
  23.5 3.4 %all-to-all-start.1 = ((bf16[8,16,1024]{2,1,0:T(8,128)(2,1)}), bf16[8,16,1024]{2,1,0:T(8,128)(2,1)S(1)}, u32[]{:S(2)}, u32[]{:S(2)}) async-start(bf16[8,16,1024]{2,1,0:T(8,128)(2,1)} %broadcast_select_fusion), calls=%async_computation.1 | async-start | bytes 524288 | tf_op jit(solution)/shard_map/all_to_all | solution.py:61
  26.9 0.9 %copy.53 = f32[128,8,64]{0,2,1:T(8,128)} copy(f32[128,8,64]{2,0,1:T(8,128)S(1)} %convert_bitcast_fusion) | data formatting | bytes 524288 | tf_op jit(solution)/shard_map/convert_element_type | solution.py:19
  27.8 0.0 copy-done.1
  27.8 0.0 copy-start.7
  27.8 2.6 %copy.58 = bf16[1024,1024]{0,1:T(8,128)(2,1)} copy(bf16[1024,1024]{1,0:T(8,128)(2,1)S(1)} %copy-done.1) | data formatting | bytes 4194304 | tf_op args[8]
  30.4 0.0 copy-done.7
  30.4 0.1 reshape.190
  30.5 0.7 %gather_fusion.3 = bf16[128,64]{1,0:T(8,128)(2,1)S(1)} fusion(bf16[128,64]{1,0:T(8,128)(2,1)S(1)} %bitcast.55, s32[1024]{0:T(1024)S(1)} %pad_clamp_fusion), kind=kCustom, calls=%fused_computation.3 | custom fusion | bytes 33280 | tf_op jit(solution)/shard_map/gather | solution.py:65
  31.2 0.1 copy.61
  31.3 2.4 %all-to-all-done.1 = bf16[8,16,1024]{2,1,0:T(8,128)(2,1)S(1)} async-done(((bf16[8,16,1024]{2,1,0:T(8,128)(2,1)}), bf16[8,16,1024]{2,1,0:T(8,128)(2,1)S(1)}, u32[]{:S(2)}, u32[]{:S(2)}) %all-to-all-start.1) | async-done | bytes 262176 | tf_op jit(solution)/shard_map/all_to_all | solution.py:61
  33.7 0.9 %gather_fusion.1 = bf16[128,1024]{1,0:T(8,128)(2,1)S(1)} fusion(bf16[128,1024]{1,0:T(8,128)(2,1)S(1)} %bitcast.54, s32[1024]{0:T(1024)S(1)} %pad_clamp_fusion), kind=kCustom, calls=%fused_computation.1 | custom fusion | bytes 524800 | tf_op jit(solution)/shard_map/gather | solution.py:64
  34.6 0.1 copy.57
  34.7 0.0 copy-start.2
  34.8 1.7 %multiply_convert_fusion.1 = bf16[128,8,16,64]{0,3,2,1:T(8,128)(2,1)S(1)} fusion(f32[128,16,64]{0,2,1:T(8,128)S(1)} %broadcast_multiply_fusion, f32[128,8,64]{0,2,1:T(8,128)} %copy.53), kind=kLoop, calls=%fused_computation.7 | loop fusion | flops 2097152 | bytes 2883584 | tf_op jit(solution)/shard_map/convert_element_type | solution.py:19
  36.5 0.0 copy-done.2
  36.5 2.4 %multiply_convert_fusion = bf16[128,8,16,64]{0,3,2,1:T(8,128)(2,1)S(1)} fusion(bf16[128,8,1024,1]{0,2,3,1:T(8,128)(2,1)S(1)} %bitcast.58, bf16[16,64,1024,1]{2,1,0,3:T(8,128)(2,1)S(1)} %bitcast.57, f32[128,64]{0,1:T(8,128)S(1)} %convert_element_type.61), kind=kOutput, calls=%fused_computation.6 | convolution fusion | flops 2149580800 | bytes 6324224 | tf_op jit(solution)/shard_map/dot_general | solution.py:20
  38.8 0.0 copy-start.4
  38.9 0.0 copy-start.5
  38.9 2.4 %multiply_reduce_fusion = f32[128,8,64]{0,2,1:T(8,128)S(1)} fusion(bf16[128,8,1024,1]{0,2,3,1:T(8,128)(2,1)S(1)} %bitcast.67, bf16[16,64,1024,1]{2,1,0,3:T(8,128)(2,1)S(1)} %bitcast.56, f32[128,16,64]{0,2,1:T(8,128)S(1)} %broadcast_multiply_fusion), kind=kOutput, calls=%fused_computation.5 | convolution fusion | flops 2149515264 | bytes 4980736 | tf_op jit(solution)/shard_map/dot_general | solution.py:26
  41.3 0.0 copy-start.3
  41.3 0.2 copy.63
  41.5 0.1 reshape.131
  41.6 0.0 copy-done.4
  41.6 0.0 copy-done.5
  41.6 0.3 convolution_bitcast_fusion
  41.9 0.2 copy-done.3
  42.2 1.0 %fusion.1 = (f32[8]{0:T(128)S(1)}, f32[8192]{0:T(1024)S(1)}, f32[8,8192]{1,0:T(8,128)}) fusion(f32[1,8,64,128]{3,2,1,0:T(8,128)S(1)} %convolution_bitcast_fusion, bf16[8,8192]{1,0:T(8,128)(2,1)S(1)} %copy-done.3), kind=kLoop, calls=%fused_computation.16 | loop fusion | flops 319480 | bytes 688160 | tf_op jit(solution)/shard_map/reduce_sum | solution.py:77
  43.2 12.4 %psum.7 = f32[8]{0:T(128)} all-reduce(f32[8]{0:T(128)S(1)} %get-tuple-element.3), channel_id=1, replica_groups=mesh['surf'=8,'probe'=4] {'surf'}, use_global_device_ids=true, to_apply=%region_6.7 | all-reduce | flops 8 | bytes 64 | tf_op jit(solution)/shard_map/psum | solution.py:77
  55.6 13.6 %all-gather = f32[32768]{0:T(1024)S(1)} all-gather(f32[8192]{0:T(1024)S(1)} %get-tuple-element.4), channel_id=2, replica_groups=mesh['surf'=8,'probe'=4] {'probe'}, dimensions={0}, use_global_device_ids=true | all-gather | bytes 163840 | tf_op jit(solution)/shard_map/all_gather | solution.py:76
  69.2 0.1 reduce_sum.48
  69.3 0.6 broadcast_multiply_fusion.1
  (9 shorter events, 0.2 us)
Async XLA Ops:
  0.6 18.2 %copy-start = (bf16[128,1024]{1,0:T(8,128)(2,1)S(1)}, bf16[128,1024]{1,0:T(8,128)(2,1)}, u32[]{:S(2)}) copy-start(bf16[128,1024]{1,0:T(8,128)(2,1)} %param.15) | copy-start | bytes 786436
  0.6 10.7 %copy-start.6 = (bf16[128,64]{0,1:T(8,128)(2,1)S(1)}, bf16[128,64]{0,1:T(8,128)(2,1)}, u32[]{:S(2)}) copy-start(bf16[128,64]{0,1:T(8,128)(2,1)} %param.16) | copy-start | bytes 49156
  4.0 9.8 %all-to-all-start = ((s32[8,1,16]{2,1,0:T(1,128)}), s32[8,1,16]{2,1,0:T(1,128)S(1)}, u32[]{:S(2)}, u32[]{:S(2)}) async-start(s32[8,1,16]{2,1,0:T(1,128)} %bitcast.3), calls=%async_computation | async-start | bytes 8192 | tf_op jit(solution)/shard_map/all_to_all | solution.py:55
  15.4 8.0 %all-to-all-start.2 = ((bf16[8,2,512]{2,1,0:T(2,128)(2,1)}), bf16[8,2,512]{2,1,0:T(2,128)(2,1)S(1)}, u32[]{:S(2)}, u32[]{:S(2)}) async-start(bf16[8,2,512]{2,1,0:T(2,128)(2,1)} %reshape.189), calls=%async_computation.2 | async-start | bytes 32768 | tf_op jit(solution)/shard_map/all_to_all | solution.py:62
  18.8 9.0 %copy-start.1 = (bf16[1024,1024]{1,0:T(8,128)(2,1)S(1)}, bf16[1024,1024]{1,0:T(8,128)(2,1)}, u32[]{:S(2)}) copy-start(bf16[1024,1024]{1,0:T(8,128)(2,1)} %param.17) | copy-start | bytes 6291460
  23.5 10.3 %all-to-all-start.1 = ((bf16[8,16,1024]{2,1,0:T(8,128)(2,1)}), bf16[8,16,1024]{2,1,0:T(8,128)(2,1)S(1)}, u32[]{:S(2)}, u32[]{:S(2)}) async-start(bf16[8,16,1024]{2,1,0:T(8,128)(2,1)} %broadcast_select_fusion), calls=%async_computation.1 | async-start | bytes 524288 | tf_op jit(solution)/shard_map/all_to_all | solution.py:61
  27.8 2.6 %copy-start.7 = (s32[128]{0:T(128)S(1)}, s32[128]{0:T(128)}, u32[]{:S(2)}) copy-start(s32[128]{0:T(128)} %param.14) | copy-start | bytes 1540
  34.7 1.7 %copy-start.2 = (bf16[1024,1024]{0,1:T(8,128)(2,1)S(1)}, bf16[1024,1024]{0,1:T(8,128)(2,1)}, u32[]{:S(2)}) copy-start(bf16[1024,1024]{0,1:T(8,128)(2,1)} %copy.58) | copy-start | bytes 6291460
  38.8 2.8 %copy-start.4 = (f32[8192]{0:T(1024)S(1)}, f32[8192]{0:T(1024)}, u32[]{:S(2)}) copy-start(f32[8192]{0:T(1024)} %param.10) | copy-start | bytes 98308
  38.9 2.8 %copy-start.5 = (bf16[128,128]{1,0:T(8,128)(2,1)S(1)}, bf16[128,128]{1,0:T(8,128)(2,1)}, u32[]{:S(2)}) copy-start(bf16[128,128]{1,0:T(8,128)(2,1)} %param.11) | copy-start | bytes 98308
  41.3 0.9 %copy-start.3 = (bf16[8,8192]{1,0:T(8,128)(2,1)S(1)}, bf16[8,8192]{1,0:T(8,128)(2,1)}, u32[]{:S(2)}) copy-start(bf16[8,8192]{1,0:T(8,128)(2,1)} %param.9) | copy-start | bytes 393220
